TPU v7x, 128 devices: a whole 4x4x4 slice. The times are simulated.
128 devices in a mesh: row: 8 (over z, core), col: 16 (over x, y).
Axes of the slice: x: 4, y: 4, z: 4, core: 2. Of those that a mesh axis runs over, the one named last changes fastest.
Arguments:
- edge_code: int32 [128, 4096], P(('row', 'col')), may hold values from 0 to 1572863
- edge_weight: bfloat16 [128, 4096], P(('row', 'col')), may hold values from 1 to 64
- edge_count: int32 [128, 128], P(('row', 'col')), may hold values from 0 to 32, as said below
- tile_blocks: int32 [128, 4, 2], P(('row', 'col')), may hold values from 0 to 127
- hub_blocks: int32 [8, 2, 2], P('row'), may hold values from 0 to 127
- node_degree: float32 [128, 512], P(('row', 'col')), may hold values from 1 to 16
Outputs:
- owned_tiles: float32 [512, 512, 512], P(('row', 'col'))
- hub_tiles: float32 [8192, 512], P(('row', 'col'))
Inputs may be any that keep to these rules, and one draw needn't show every extreme that they name: `edge_count`: at most 32 used slots from one device to another; in every draw some device receives 32 used slots from every device, and the loads of destinations differ widely.
All inputs are finite; a program needn't handle non-finite values.
Results may differ from a plain program's by a relative error of at most 0.0003.
Values may be sent and summed in bfloat16 or wider, within the bound.
A program may use at most 64 MiB of HBM per device.

v0:
```python
import jax
import jax.numpy as jnp
from jax import lax
from jax.sharding import Mesh
from jax.sharding import PartitionSpec as P

TILE = 512
TILES_DEV = 4
HUBS = 2
CAP = 32
ROW = ("row_0", "row_1")
COL = ("col_0", "col_1")
ROW_COL = ("row_0", "row_1", "col_0", "col_1")


def cut_along(x, dim, size):
    before, after = (x.shape[:dim], x.shape[dim + 1 :])
    return jnp.moveaxis(x.reshape(*before, size, -1, *after), dim, 0)


def in_order(blocks, dim):
    blocks = jnp.moveaxis(blocks, 0, dim)
    dims = blocks.shape
    return blocks.reshape(*dims[:dim], dims[dim] * dims[dim + 1], *dims[dim + 2 :])


def one_exchange(x, axis, axes, splits, concats):
    sizes = [lax.axis_size(a) for a in axes]
    blocks = cut_along(x, splits[0], sizes[0])
    blocks = jnp.moveaxis(cut_along(blocks, splits[1] + 1, sizes[1]), 0, 1)
    inside = blocks.shape[2:]
    blocks = blocks.reshape(-1, *inside)
    blocks = lax.all_to_all(blocks, axis, split_axis=0, concat_axis=0, tiled=True)
    blocks = in_order(blocks.reshape(*sizes, *inside), concats[0] + 1)
    return in_order(blocks, concats[1])


def stacked_from(x, axes, order):
    blocks = x[None]
    for k in order:
        blocks = lax.all_gather(blocks, axes[k], axis=0, tiled=True)
    block = [lax.axis_size(axes[k]) for k in reversed(order)]
    blocks = blocks.reshape(*block, *x.shape)
    turned = sorted(range(len(order)), key=lambda place: order[len(order) - 1 - place])
    return blocks.transpose(*turned, *range(len(order), blocks.ndim)).reshape(-1, *x.shape)


def gather_axes(x, axes, order, dim):
    return in_order(stacked_from(x, axes, order), dim)


def sum_at_owner(x, axis, dim):
    size = lax.axis_size(axis)
    blocks = lax.all_to_all(cut_along(x, dim, size), axis, 0, 0, tiled=True)
    return jnp.sum(blocks.astype(jnp.float32), axis=0)


def lookup(indices, degrees):
    selector = (indices[:, None] == jnp.arange(degrees.shape[0], dtype=jnp.int32)[None, :]).astype(
        jnp.float32
    )
    return jnp.dot(selector, degrees, precision=lax.Precision.HIGHEST)


def accumulate_rows(edge_codes, weights, row_count):
    total_edges = edge_codes.shape[0]
    block = 512
    row_keys = jnp.arange(row_count, dtype=jnp.int32)
    col_keys = jnp.arange(TILE, dtype=jnp.int32)

    def step_block(turn, totals):
        start = turn * block
        part_codes = lax.dynamic_slice_in_dim(edge_codes, start, block)
        part_weights = lax.dynamic_slice_in_dim(weights, start, block)
        left_side = jnp.where(
            part_codes[:, None] // TILE == row_keys[None, :],
            part_weights[:, None],
            jnp.zeros((), jnp.bfloat16),
        )
        right_side = (part_codes[:, None] % TILE == col_keys[None, :]).astype(jnp.bfloat16)
        return totals + lax.dot_general(
            left_side, right_side, (((0,), (0,)), ((), ())), preferred_element_type=jnp.float32
        )

    return lax.fori_loop(
        0, total_edges // block, step_block, jnp.zeros((row_count, TILE), jnp.float32)
    )


def shards(edge_code, edge_weight, edge_count, tile_blocks, hub_blocks, node_degree):
    n_row = lax.axis_size(ROW)
    n_col = lax.axis_size(COL)
    devices = n_row * n_col
    edge_codes, weights, counts = (
        one_exchange(edge_code.reshape(n_row, n_col, CAP), ROW_COL, (ROW, COL), (0, 1), (0, 1)),
        one_exchange(edge_weight.reshape(n_row, n_col, CAP), ROW_COL, (ROW, COL), (0, 1), (0, 1)),
        one_exchange(edge_count.reshape(n_row, n_col, 1), ROW_COL, (ROW, COL), (0, 1), (0, 1)),
    )
    edge_codes = edge_codes.reshape(devices, CAP)
    weights = weights.reshape(devices, CAP)
    counts = counts.reshape(devices, 1)
    usable = jnp.arange(CAP, dtype=jnp.int32)[None, :] < counts
    weights = jnp.where(usable, weights, jnp.zeros((), jnp.bfloat16)).reshape(-1)
    edge_codes = edge_codes.reshape(-1)
    degrees = gather_axes(node_degree, ROW_COL, (0, 2, 3, 1), 0)
    scaling = jnp.sum(degrees) / degrees.size
    slab_rows = HUBS * TILE // n_col
    offset = lax.axis_index(COL) * slab_rows
    totals = accumulate_rows(edge_codes, weights, (TILES_DEV + HUBS) * TILE)
    owned = totals[: TILES_DEV * TILE].reshape(TILES_DEV, TILE, TILE)
    summed = sum_at_owner(totals[TILES_DEV * TILE :].astype(jnp.bfloat16), COL, 0)
    blocks = tile_blocks[0]
    row_degree = lookup(blocks[:, 0], degrees)
    col_degree = lookup(blocks[:, 1], degrees)
    owned_tiles = jnp.log(
        jnp.maximum(scaling * owned / (row_degree[:, :, None] * col_degree[:, None, :]), 1.0)
    )
    hub_rows = lookup(hub_blocks[0][:, 0], degrees).reshape(-1)
    hub_row_degree = lax.dynamic_slice_in_dim(hub_rows, offset, slab_rows)
    hub_cols = lookup(hub_blocks[0][:, 1], degrees)
    hub_index = (offset + jnp.arange(slab_rows, dtype=jnp.int32)) // TILE
    selector = (hub_index[:, None] == jnp.arange(HUBS, dtype=jnp.int32)[None, :]).astype(
        jnp.float32
    )
    hub_col_degree = jnp.dot(selector, hub_cols, precision=lax.Precision.HIGHEST)
    hub_tiles = jnp.log(
        jnp.maximum(scaling * summed / (hub_row_degree[:, None] * hub_col_degree), 1.0)
    )
    return (owned_tiles, hub_tiles)


def solution(mesh):
    split = Mesh(mesh.devices.reshape(4, 2, 4, 4), ("row_0", "row_1", "col_0", "col_1"))
    placed = (
        P(ROW_COL, None),
        P(ROW_COL, None),
        P(ROW_COL, None),
        P(ROW_COL, None, None),
        P(ROW, None, None),
        P(ROW_COL, None),
    )
    return jax.shard_map(
        shards,
        mesh=split,
        in_specs=placed,
        out_specs=(P(ROW_COL, None, None), P(ROW_COL, None)),
        check_vma=False,
    )
```

profile of v0, /device:TPU:0, one launch (start us, length us, event | category | flops | bytes accessed | tf_op | source)
XLA Modules:
  0.0 174.7 jit_solution(8583765645140113446)
XLA Ops:
  0.6 1.4 copy.16
  2.0 11.2 %all-to-all-start.1 = ((s32[128,1,1,1]{3,2,1,0:T(1,128)}), s32[128,1,1,1]{3,2,1,0:T(1,128)S(1)}, u32[]{:S(2)}, u32[]{:S(2)}) async-start(s32[128,1,1,1]{3,2,1,0:T(1,128)} %copy.16), calls=%async_computation.1 | async-start | bytes 131072 | tf_op jit(solution)/shard_map/all_to_all | solution.py:33
  13.2 0.8 slice_bitcast_fusion.1
  14.0 1.0 slice_reduce_fusion.1
  15.0 11.1 %all-gather.4 = f32[4,1,512]{2,1,0:T(1,128)S(1)} all-gather(f32[1,1,512]{2,1,0:T(1,128)} %bitcast.64), channel_id=2, replica_groups=mesh['row_0'=4,'row_1'=2,'col_0'=4,'col_1'=4] {'row_0'}, dimensions={0}, use_global_device_ids=true | all-gather | bytes 10240 | tf_op jit(solution)/shard_map/all_gather | solution.py:41
  26.1 12.2 %all-gather.5 = f32[4,4,512]{2,1,0:T(4,128)S(1)} all-gather(f32[1,4,512]{2,1,0:T(4,128)S(1)} %copy.14), channel_id=3, replica_groups=mesh['row_0'=4,'row_1'=2,'col_0'=4,'col_1'=4] {'col_0'}, dimensions={0}, use_global_device_ids=true | all-gather | bytes 40960 | tf_op jit(solution)/shard_map/all_gather | solution.py:41
  38.3 0.5 broadcast.148
  38.9 1.4 reduce.13
  40.3 0.7 reshape_transpose_transpose_reshape_reshape_reshape.9
  41.0 12.4 %all-gather.2 = f32[64,512]{1,0:T(8,128)S(1)} all-gather(f32[16,512]{1,0:T(8,128)S(1)} %reshape.108), channel_id=4, replica_groups=mesh['row_0'=4,'row_1'=2,'col_0'=4,'col_1'=4] {'col_1'}, dimensions={0}, use_global_device_ids=true | all-gather | bytes 163840 | tf_op jit(solution)/shard_map/all_gather | solution.py:41
  53.4 2.0 %all-gather.3 = f32[128,512]{1,0:T(8,128)S(1)} all-gather(f32[64,512]{1,0:T(8,128)S(1)} %all-gather.2), channel_id=5, replica_groups=mesh['row_0'=4,'row_1'=2,'col_0'=4,'col_1'=4] {'row_1'}, dimensions={0}, use_global_device_ids=true | all-gather | bytes 393216 | tf_op jit(solution)/shard_map/all_gather | solution.py:41
  55.4 0.2 copy.22
  55.6 0.1 reshape_reshape.8
  55.7 0.2 fusion.18
  55.9 0.2 convolution_bitcast_fusion
  56.1 0.2 fusion.17
  56.4 0.2 fusion.16
  56.6 0.8 reduce.6
  57.4 0.7 reshape_transpose_transpose_reshape_reshape_reshape.12
  58.1 0.7 reduce_sum.18
  59.5 0.1 dynamic_slice.23
  59.6 7.7 %all-to-all-start.2 = ((bf16[128,1,1,32]{3,2,1,0:T(2,128)(2,1)}), bf16[128,1,1,32]{3,2,1,0:T(2,128)(2,1)S(1)}, u32[]{:S(2)}, u32[]{:S(2)}) async-start(bf16[128,1,1,32]{3,2,1,0:T(2,128)(2,1)} %reshape_transpose_transpose_reshape_reshape_reshape.12), calls=%async_computation.2 | async-start | bytes 131072 | tf_op jit(solution)/shard_map/all_to_all | solution.py:33
  67.3 2.4 %reduce.5 = s32[128]{0:T(128)S(1)} reduce(s32[128,1,1,1]{3,2,1,0:T(1,128)S(1)} %all-to-all-done.1, s32[]{:T(128)} %constant.122.clone.1), dimensions={1,2,3}, to_apply=%all_to_all.13.reduce_sub_computation | reduce | bytes 1028 | tf_op jit(solution)/shard_map/all_to_all | solution.py:33
  69.7 0.1 reshape.93
  69.8 0.1 lt.51
  69.8 0.1 iota_compare_fusion.3
  69.9 0.1 lt.54
  70.0 6.8 %all-to-all-done.2 = bf16[128,1,1,32]{3,2,1,0:T(2,128)(2,1)S(1)} async-done(((bf16[128,1,1,32]{3,2,1,0:T(2,128)(2,1)}), bf16[128,1,1,32]{3,2,1,0:T(2,128)(2,1)S(1)}, u32[]{:S(2)}, u32[]{:S(2)}) %all-to-all-start.2) | async-done | bytes 8224 | tf_op jit(solution)/shard_map/all_to_all | solution.py:33
  76.8 4.6 %all-to-all-start = ((s32[128,1,1,32]{3,2,1,0:T(1,128)}), s32[128,1,1,32]{3,2,1,0:T(1,128)S(1)}, u32[]{:S(2)}, u32[]{:S(2)}) async-start(s32[128,1,1,32]{3,2,1,0:T(1,128)} %bitcast.2), calls=%async_computation | async-start | bytes 131072 | tf_op jit(solution)/shard_map/all_to_all | solution.py:33
  81.4 0.1 reshape_reshape.7
  81.5 9.3 %all-to-all-done = s32[128,1,1,32]{3,2,1,0:T(1,128)S(1)} async-done(((s32[128,1,1,32]{3,2,1,0:T(1,128)}), s32[128,1,1,32]{3,2,1,0:T(1,128)S(1)}, u32[]{:S(2)}, u32[]{:S(2)}) %all-to-all-start) | async-done | bytes 16416 | tf_op jit(solution)/shard_map/all_to_all | solution.py:33
  90.9 0.1 reshape_reshape_reshape.3
  90.9 58.6 %while.16 = (s32[]{:T(128)}, f32[3072,512]{1,0:T(8,128)}, s32[4096]{0:T(1024)S(1)}, bf16[4096]{0:T(1024)(128)(2,1)S(1)}, s32[]{:T(128)}, /*index=5*/s32[]{:T(128)}, s32[]{:T(128)}, s32[]{:T(128)}) while((s32[]{:T(128)}, f32[3072,512]{1,0:T(8,128)}, s32[4096]{0:T(1024)S(1)}, bf16[4096]{0:T(1024)(128)(2,1)S(1)}, s32[]{:T(128)}, ...), condition=%wide.region_2.3_spmd.clone, body=%wide.region_1.2_spmd.clone.sunk | while | flops 1617176064 | bytes 12596381 | solution.py:85
  91.0 0.1 dynamic_slice.35
  91.0 0.1 add_select_fusion.3
  91.1 4.7 %select_add_fusion.2 = f32[3072,512]{1,0:T(8,128)} fusion(f32[3072,512]{1,0:T(8,128)} %get-tuple-element.231, s32[512]{0:T(512)S(1)} %get-tuple-element.220, pred[]{:T(512)S(6)} %compare.23, bf16[512]{0:T(512)(128)(2,1)S(1)} %dynamic_slice.35, s32[512]{0:T(512)S(1)} %get-tuple-element.221), kind=kOutput, calls=%fused_computation.3.clone.1 | convolution fusion | flops 1617166336 | bytes 12588033 | tf_op jit(solution)/shard_map/while/body/eval_jaxpr/dot_general | solution.py:81
  95.9 0.1 dynamic_slice.35
  95.9 0.1 add_select_fusion.3
  96.0 7.5 %select_add_fusion.2 = f32[3072,512]{1,0:T(8,128)} fusion(f32[3072,512]{1,0:T(8,128)} %get-tuple-element.231, s32[512]{0:T(512)S(1)} %get-tuple-element.220, pred[]{:T(512)S(6)} %compare.23, bf16[512]{0:T(512)(128)(2,1)S(1)} %dynamic_slice.35, s32[512]{0:T(512)S(1)} %get-tuple-element.221), kind=kOutput, calls=%fused_computation.3.clone.1 | convolution fusion | flops 1617166336 | bytes 12588033 | tf_op jit(solution)/shard_map/while/body/eval_jaxpr/dot_general | solution.py:81
  103.5 0.1 dynamic_slice.35
  103.6 0.1 add_select_fusion.3
  103.7 7.5 %select_add_fusion.2 = f32[3072,512]{1,0:T(8,128)} fusion(f32[3072,512]{1,0:T(8,128)} %get-tuple-element.231, s32[512]{0:T(512)S(1)} %get-tuple-element.220, pred[]{:T(512)S(6)} %compare.23, bf16[512]{0:T(512)(128)(2,1)S(1)} %dynamic_slice.35, s32[512]{0:T(512)S(1)} %get-tuple-element.221), kind=kOutput, calls=%fused_computation.3.clone.1 | convolution fusion | flops 1617166336 | bytes 12588033 | tf_op jit(solution)/shard_map/while/body/eval_jaxpr/dot_general | solution.py:81
  111.2 0.1 dynamic_slice.35
  111.3 0.1 add_select_fusion.3
  111.4 7.5 %select_add_fusion.2 = f32[3072,512]{1,0:T(8,128)} fusion(f32[3072,512]{1,0:T(8,128)} %get-tuple-element.231, s32[512]{0:T(512)S(1)} %get-tuple-element.220, pred[]{:T(512)S(6)} %compare.23, bf16[512]{0:T(512)(128)(2,1)S(1)} %dynamic_slice.35, s32[512]{0:T(512)S(1)} %get-tuple-element.221), kind=kOutput, calls=%fused_computation.3.clone.1 | convolution fusion | flops 1617166336 | bytes 12588033 | tf_op jit(solution)/shard_map/while/body/eval_jaxpr/dot_general | solution.py:81
  118.9 0.1 dynamic_slice.35
  119.0 0.1 add_select_fusion.3
  119.0 7.5 %select_add_fusion.2 = f32[3072,512]{1,0:T(8,128)} fusion(f32[3072,512]{1,0:T(8,128)} %get-tuple-element.231, s32[512]{0:T(512)S(1)} %get-tuple-element.220, pred[]{:T(512)S(6)} %compare.23, bf16[512]{0:T(512)(128)(2,1)S(1)} %dynamic_slice.35, s32[512]{0:T(512)S(1)} %get-tuple-element.221), kind=kOutput, calls=%fused_computation.3.clone.1 | convolution fusion | flops 1617166336 | bytes 12588033 | tf_op jit(solution)/shard_map/while/body/eval_jaxpr/dot_general | solution.py:81
  126.6 0.1 dynamic_slice.35
  126.6 0.1 add_select_fusion.3
  126.7 7.5 %select_add_fusion.2 = f32[3072,512]{1,0:T(8,128)} fusion(f32[3072,512]{1,0:T(8,128)} %get-tuple-element.231, s32[512]{0:T(512)S(1)} %get-tuple-element.220, pred[]{:T(512)S(6)} %compare.23, bf16[512]{0:T(512)(128)(2,1)S(1)} %dynamic_slice.35, s32[512]{0:T(512)S(1)} %get-tuple-element.221), kind=kOutput, calls=%fused_computation.3.clone.1 | convolution fusion | flops 1617166336 | bytes 12588033 | tf_op jit(solution)/shard_map/while/body/eval_jaxpr/dot_general | solution.py:81
  134.2 0.1 dynamic_slice.35
  134.3 0.1 add_select_fusion.3
  134.4 7.5 %select_add_fusion.2 = f32[3072,512]{1,0:T(8,128)} fusion(f32[3072,512]{1,0:T(8,128)} %get-tuple-element.231, s32[512]{0:T(512)S(1)} %get-tuple-element.220, pred[]{:T(512)S(6)} %compare.23, bf16[512]{0:T(512)(128)(2,1)S(1)} %dynamic_slice.35, s32[512]{0:T(512)S(1)} %get-tuple-element.221), kind=kOutput, calls=%fused_computation.3.clone.1 | convolution fusion | flops 1617166336 | bytes 12588033 | tf_op jit(solution)/shard_map/while/body/eval_jaxpr/dot_general | solution.py:81
  141.9 0.1 dynamic_slice.35
  142.0 0.1 add_select_fusion.3
  142.1 7.5 %select_add_fusion.2 = f32[3072,512]{1,0:T(8,128)} fusion(f32[3072,512]{1,0:T(8,128)} %get-tuple-element.231, s32[512]{0:T(512)S(1)} %get-tuple-element.220, pred[]{:T(512)S(6)} %compare.23, bf16[512]{0:T(512)(128)(2,1)S(1)} %dynamic_slice.35, s32[512]{0:T(512)S(1)} %get-tuple-element.221), kind=kOutput, calls=%fused_computation.3.clone.1 | convolution fusion | flops 1617166336 | bytes 12588033 | tf_op jit(solution)/shard_map/while/body/eval_jaxpr/dot_general | solution.py:81
  149.6 2.7 %slice.32 = bf16[1024,512]{1,0:T(8,128)(2,1)} slice(f32[3072,512]{1,0:T(8,128)} %get-tuple-element.159), slice={[2048:3072], [0:512]} | slice | bytes 2097152 | tf_op jit(solution)/shard_map/slice | solution.py:111
  152.3 3.7 %all-to-all-start.3 = ((bf16[16,64,512]{2,1,0:T(8,128)(2,1)}), bf16[16,64,512]{2,1,0:T(8,128)(2,1)S(1)}, u32[]{:S(2)}, u32[]{:S(2)}) async-start(bf16[16,64,512]{2,1,0:T(8,128)(2,1)} %bitcast.19), calls=%async_computation.3 | async-start | bytes 2097152 | tf_op jit(solution)/shard_map/all_to_all | solution.py:54
  156.0 2.7 %slice_multiply_fusion = f32[2048,512]{1,0:T(8,128)S(1)} fusion(f32[3072,512]{1,0:T(8,128)} %get-tuple-element.159, f32[]{:T(128)S(6)} %div.35), kind=kLoop, calls=%fused_computation.20 | loop fusion | flops 1048576 | bytes 8388612 | tf_op jit(solution)/shard_map/mul | solution.py:116
  158.7 2.7 %maximum_log_fusion = f32[4,512,512]{2,1,0:T(8,128)} fusion(f32[4,512,512]{2,1,0:T(8,128)S(1)} %bitcast.56, f32[4,512]{1,0:T(4,128)S(1)} %fusion.17, f32[4,512]{1,0:T(4,128)S(1)} %fusion.16), kind=kLoop, calls=%fused_computation.19 | loop fusion | flops 3145728 | bytes 8404992 | tf_op jit(solution)/shard_map/log | solution.py:115
  161.3 12.3 %all-to-all-done.3 = bf16[16,64,512]{2,1,0:T(8,128)(2,1)S(1)} async-done(((bf16[16,64,512]{2,1,0:T(8,128)(2,1)}), bf16[16,64,512]{2,1,0:T(8,128)(2,1)S(1)}, u32[]{:S(2)}, u32[]{:S(2)}) %all-to-all-start.3) | async-done | bytes 1048608 | tf_op jit(solution)/shard_map/all_to_all | solution.py:54
  173.7 0.1 convert_reduce_fusion
  173.8 0.9 fusion.14
  (9 shorter events, 0.1 us)
Async XLA Ops:
  2.0 57.6 %all-to-all-start.1 = ((s32[128,1,1,1]{3,2,1,0:T(1,128)}), s32[128,1,1,1]{3,2,1,0:T(1,128)S(1)}, u32[]{:S(2)}, u32[]{:S(2)}) async-start(s32[128,1,1,1]{3,2,1,0:T(1,128)} %copy.16), calls=%async_computation.1 | async-start | bytes 131072 | tf_op jit(solution)/shard_map/all_to_all | solution.py:33
  59.6 17.2 %all-to-all-start.2 = ((bf16[128,1,1,32]{3,2,1,0:T(2,128)(2,1)}), bf16[128,1,1,32]{3,2,1,0:T(2,128)(2,1)S(1)}, u32[]{:S(2)}, u32[]{:S(2)}) async-start(bf16[128,1,1,32]{3,2,1,0:T(2,128)(2,1)} %reshape_transpose_transpose_reshape_reshape_reshape.12), calls=%async_computation.2 | async-start | bytes 131072 | tf_op jit(solution)/shard_map/all_to_all | solution.py:33
  76.8 14.0 %all-to-all-start = ((s32[128,1,1,32]{3,2,1,0:T(1,128)}), s32[128,1,1,32]{3,2,1,0:T(1,128)S(1)}, u32[]{:S(2)}, u32[]{:S(2)}) async-start(s32[128,1,1,32]{3,2,1,0:T(1,128)} %bitcast.2), calls=%async_computation | async-start | bytes 131072 | tf_op jit(solution)/shard_map/all_to_all | solution.py:33
  152.3 21.3 %all-to-all-start.3 = ((bf16[16,64,512]{2,1,0:T(8,128)(2,1)}), bf16[16,64,512]{2,1,0:T(8,128)(2,1)S(1)}, u32[]{:S(2)}, u32[]{:S(2)}) async-start(bf16[16,64,512]{2,1,0:T(8,128)(2,1)} %bitcast.19), calls=%async_computation.3 | async-start | bytes 2097152 | tf_op jit(solution)/shard_map/all_to_all | solution.py:54
where the time goes:
time: 176 us; the launch traced here: 175 us
  matrix products  59.2 us (34%)
  blocking collectives  37.8 us (21%)
  waiting for transfers between devices  28.4 us (16%)
  starting transfers between devices  27.1 us (15%)
  other arithmetic  11.5 us (7%)
  local copies, waits for them, and re-layouts  9.26 us (5%)
    dot_general x8, matrix products, step_block(): lax.dot_general(left_side, right_side, (((0,), (0,)), ((), ())), preferre...  57.3 us
    all_gather x4, blocking collectives, stacked_from(): blocks = lax.all_gather(blocks, axes[k], axis=0, tiled=True)  37.8 us
    all_to_all x3, starting transfers between devices, one_exchange(): lax.all_to_all(blocks, axis, split_axis=0, concat_axis=0, tiled=True)  23.5 us
    all_to_all x3, waiting for transfers between devices, one_exchange(): lax.all_to_all(blocks, axis, split_axis=0, concat_axis=0, tiled=True)  16.1 us
    all_to_all x1, waiting for transfers between devices, sum_at_owner(): blocks = lax.all_to_all(cut_along(x, dim, size), axis, 0, 0, tiled=True)  12.3 us
    all_to_all x1, starting transfers between devices, sum_at_owner(): blocks = lax.all_to_all(cut_along(x, dim, size), axis, 0, 0, tiled=True)  3.65 us
  transfers between devices with their start and end apart: 4, of which 3 were waited for; matrix products, arithmetic and copies ran while one was open for 9% of the time, Pallas kernels for 0%

commit v1 on v0

--- a/solution.py
+++ b/solution.py
@@ -38,7 +38,9 @@
 def stacked_from(x, axes, order):
     blocks = x[None]
     for k in order:
-        blocks = lax.all_gather(blocks, axes[k], axis=0, tiled=True)
+        blocks = jnp.concatenate(
+            lax.all_to_all(jnp.stack([blocks] * lax.axis_size(axes[k])), axes[k], 0, 0), axis=0
+        )
     block = [lax.axis_size(axes[k]) for k in reversed(order)]
     blocks = blocks.reshape(*block, *x.shape)
     turned = sorted(range(len(order)), key=lambda place: order[len(order) - 1 - place])

time: 176 us -> 166 us (0.943)
  blocking collectives: 37.8 us -> 3.94 us
  waiting for transfers between devices: 28.4 us -> 40.2 us
  starting transfers between devices: 27.1 us -> 36.6 us
  local copies, waits for them, and re-layouts: 9.26 us -> 12 us
    all_gather x4 -> x0, blocking collectives: 37.8 us -> none  [stacked_from(): blocks = lax.all_gather(blocks, axes[k], axis=0, tiled=True)]
    all_to_all x0 -> x3, starting transfers between devices: none -> 9.84 us  [stacked_from(): lax.all_to_all(jnp.stack([blocks] * lax.axis_size(axes[k])), axes[k], 0, 0)]
    all_to_all x0 -> x3, waiting for transfers between devices: none -> 8.14 us  [stacked_from(): lax.all_to_all(jnp.stack([blocks] * lax.axis_size(axes[k])), axes[k], 0, 0)]
    all_to_all x3, waiting for transfers between devices: 16.1 us -> 22.1 us  [one_exchange(): lax.all_to_all(blocks, axis, split_axis=0, concat_axis=0, tiled=True)]
    all_to_all x0 -> x1, blocking collectives: none -> 3.94 us  [stacked_from(): lax.all_to_all(jnp.stack([blocks] * lax.axis_size(axes[k])), axes[k], 0, 0)]
    another operation x0 -> x4, local copies, waits for them, and re-layouts: none -> 2.59 us  [stacked_from(): jnp.stack([blocks] * lax.axis_size(axes[k]))]
    all_to_all x1, waiting for transfers between devices: 12.3 us -> 10 us  [sum_at_owner(): blocks = lax.all_to_all(cut_along(x, dim, size), axis, 0, 0, tiled=True)]
    all_to_all x3, starting transfers between devices: 23.5 us -> 21.3 us  [one_exchange(): lax.all_to_all(blocks, axis, split_axis=0, concat_axis=0, tiled=True)]
  transfers between devices with their start and end apart: 4 -> 7, of which waited for: 3 -> 6; matrix products, arithmetic and copies ran while one was open for 9% -> 47% of each run, Pallas kernels for 0% -> 0%
where the time goes in v1:
time: 166 us; the launch traced here: 165 us
  matrix products  59.2 us (36%)
  waiting for transfers between devices  40.2 us (24%)
  starting transfers between devices  36.6 us (22%)
  local copies, waits for them, and re-layouts  12 us (7%)
  other arithmetic  11.5 us (7%)
  blocking collectives  3.94 us (2%)
    dot_general x8, matrix products, step_block(): lax.dot_general(left_side, right_side, (((0,), (0,)), ((), ())), preferre...  57.3 us
    all_to_all x3, waiting for transfers between devices, one_exchange(): lax.all_to_all(blocks, axis, split_axis=0, concat_axis=0, tiled=True)  22.1 us
    all_to_all x3, starting transfers between devices, one_exchange(): lax.all_to_all(blocks, axis, split_axis=0, concat_axis=0, tiled=True)  21.3 us
    all_to_all x1, waiting for transfers between devices, sum_at_owner(): blocks = lax.all_to_all(cut_along(x, dim, size), axis, 0, 0, tiled=True)  10 us
    all_to_all x3, starting transfers between devices, stacked_from(): lax.all_to_all(jnp.stack([blocks] * lax.axis_size(axes[k])), axes[k], 0, 0)  9.84 us
    all_to_all x3, waiting for transfers between devices, stacked_from(): lax.all_to_all(jnp.stack([blocks] * lax.axis_size(axes[k])), axes[k], 0, 0)  8.14 us
    all_to_all x1, starting transfers between devices, sum_at_owner(): blocks = lax.all_to_all(cut_along(x, dim, size), axis, 0, 0, tiled=True)  5.45 us
    all_to_all x1, blocking collectives, stacked_from(): lax.all_to_all(jnp.stack([blocks] * lax.axis_size(axes[k])), axes[k], 0, 0)  3.94 us
  transfers between devices with their start and end apart: 7, of which 6 were waited for; matrix products, arithmetic and copies ran while one was open for 47% of the time, Pallas kernels for 0%

profile of v1, /device:TPU:0, one launch (start us, length us, event | category | flops | bytes accessed | tf_op | source)
XLA Modules:
  0.0 164.8 jit_solution(16265589778900287642)
XLA Ops:
  0.6 1.4 copy.20
  2.0 11.2 %all-to-all-start.5 = ((s32[128,1,1,1]{3,2,1,0:T(1,128)}), s32[128,1,1,1]{3,2,1,0:T(1,128)S(1)}, u32[]{:S(2)}, u32[]{:S(2)}) async-start(s32[128,1,1,1]{3,2,1,0:T(1,128)} %copy.20), calls=%async_computation.5 | async-start | bytes 131072 | tf_op jit(solution)/shard_map/all_to_all | solution.py:33
  13.2 0.8 slice_bitcast_fusion.1
  14.0 8.7 %all-to-all-done.5 = s32[128,1,1,1]{3,2,1,0:T(1,128)S(1)} async-done(((s32[128,1,1,1]{3,2,1,0:T(1,128)}), s32[128,1,1,1]{3,2,1,0:T(1,128)S(1)}, u32[]{:S(2)}, u32[]{:S(2)}) %all-to-all-start.5) | async-done | bytes 544 | tf_op jit(solution)/shard_map/all_to_all | solution.py:33
  22.6 1.3 stack.12
  23.9 3.2 %all-to-all-start = ((f32[4,1,1,512]{3,2,1,0:T(1,128)}), f32[4,1,1,512]{3,2,1,0:T(1,128)S(1)}, u32[]{:S(2)}, u32[]{:S(2)}) async-start(f32[4,1,1,512]{3,2,1,0:T(1,128)} %stack.12), calls=%async_computation | async-start | bytes 16384 | tf_op jit(solution)/shard_map/all_to_all | solution.py:42
  27.2 1.0 slice_reduce_fusion.1
  28.1 0.8 reduce.5
  28.9 0.7 reshape_transpose_transpose_reshape_reshape_reshape.12
  29.6 2.8 %all-to-all-done = f32[4,1,1,512]{3,2,1,0:T(1,128)S(1)} async-done(((f32[4,1,1,512]{3,2,1,0:T(1,128)}), f32[4,1,1,512]{3,2,1,0:T(1,128)S(1)}, u32[]{:S(2)}, u32[]{:S(2)}) %all-to-all-start) | async-done | bytes 8224 | tf_op jit(solution)/shard_map/all_to_all | solution.py:42
  32.5 4.6 %all-to-all-start.6 = ((bf16[128,1,1,32]{3,2,1,0:T(2,128)(2,1)}), bf16[128,1,1,32]{3,2,1,0:T(2,128)(2,1)S(1)}, u32[]{:S(2)}, u32[]{:S(2)}) async-start(bf16[128,1,1,32]{3,2,1,0:T(2,128)(2,1)} %reshape_transpose_transpose_reshape_reshape_reshape.12), calls=%async_computation.6 | async-start | bytes 131072 | tf_op jit(solution)/shard_map/all_to_all | solution.py:33
  37.1 0.5 broadcast.155
  37.6 1.4 reduce.12
  39.0 0.7 reshape_transpose_transpose_reshape_reshape_reshape.9
  39.7 2.3 %reduce.4 = s32[128]{0:T(128)S(1)} reduce(s32[128,1,1,1]{3,2,1,0:T(1,128)S(1)} %all-to-all-done.5, s32[]{:T(128)} %constant.122.clone.1), dimensions={1,2,3}, to_apply=%all_to_all.29.reduce_sub_computation | reduce | bytes 1028 | tf_op jit(solution)/shard_map/all_to_all | solution.py:33
  42.1 0.1 reshape.101
  42.1 0.1 lt.51
  42.2 4.3 %all-to-all-done.6 = bf16[128,1,1,32]{3,2,1,0:T(2,128)(2,1)S(1)} async-done(((bf16[128,1,1,32]{3,2,1,0:T(2,128)(2,1)}), bf16[128,1,1,32]{3,2,1,0:T(2,128)(2,1)S(1)}, u32[]{:S(2)}, u32[]{:S(2)}) %all-to-all-start.6) | async-done | bytes 8224 | tf_op jit(solution)/shard_map/all_to_all | solution.py:33
  46.5 5.5 %all-to-all-start.4 = ((s32[128,1,1,32]{3,2,1,0:T(1,128)}), s32[128,1,1,32]{3,2,1,0:T(1,128)S(1)}, u32[]{:S(2)}, u32[]{:S(2)}) async-start(s32[128,1,1,32]{3,2,1,0:T(1,128)} %bitcast.2), calls=%async_computation.4 | async-start | bytes 131072 | tf_op jit(solution)/shard_map/all_to_all | solution.py:33
  52.0 0.1 iota_compare_fusion.3
  52.1 0.1 lt.54
  52.2 0.1 reshape_reshape.10
  52.3 9.1 %all-to-all-done.4 = s32[128,1,1,32]{3,2,1,0:T(1,128)S(1)} async-done(((s32[128,1,1,32]{3,2,1,0:T(1,128)}), s32[128,1,1,32]{3,2,1,0:T(1,128)S(1)}, u32[]{:S(2)}, u32[]{:S(2)}) %all-to-all-start.4) | async-done | bytes 16416 | tf_op jit(solution)/shard_map/all_to_all | solution.py:33
  61.4 0.6 stack.13
  62.1 3.3 %all-to-all-start.1 = ((f32[4,4,1,512]{3,1,2,0:T(4,128)}), f32[4,4,1,512]{3,1,2,0:T(4,128)S(1)}, u32[]{:S(2)}, u32[]{:S(2)}) async-start(f32[4,4,1,512]{3,1,2,0:T(4,128)} %stack.13), calls=%async_computation.1 | async-start | bytes 65536 | tf_op jit(solution)/shard_map/all_to_all | solution.py:42
  65.4 0.1 reshape_reshape_reshape.3
  65.4 5.3 %all-to-all-done.1 = f32[4,4,1,512]{3,1,2,0:T(4,128)S(1)} async-done(((f32[4,4,1,512]{3,1,2,0:T(4,128)}), f32[4,4,1,512]{3,1,2,0:T(4,128)S(1)}, u32[]{:S(2)}, u32[]{:S(2)}) %all-to-all-start.1) | async-done | bytes 32800 | tf_op jit(solution)/shard_map/all_to_all | solution.py:42
  70.8 0.7 stack.14
  71.4 3.3 %all-to-all-start.2 = ((f32[4,16,1,512]{3,1,2,0:T(8,128)}), f32[4,16,1,512]{3,1,2,0:T(8,128)S(1)}, u32[]{:S(2)}, u32[]{:S(2)}) async-start(f32[4,16,1,512]{3,1,2,0:T(8,128)} %stack.14), calls=%async_computation.2 | async-start | bytes 262144 | tf_op jit(solution)/shard_map/all_to_all | solution.py:42
  74.8 58.7 %while.16 = (s32[]{:T(128)}, f32[3072,512]{1,0:T(8,128)}, s32[4096]{0:T(1024)S(1)}, bf16[4096]{0:T(1024)(128)(2,1)S(1)}, s32[]{:T(128)}, /*index=5*/s32[]{:T(128)}, s32[]{:T(128)}, s32[]{:T(128)}) while((s32[]{:T(128)}, f32[3072,512]{1,0:T(8,128)}, s32[4096]{0:T(1024)S(1)}, bf16[4096]{0:T(1024)(128)(2,1)S(1)}, s32[]{:T(128)}, ...), condition=%wide.region_2.3_spmd.clone, body=%wide.region_1.2_spmd.clone.sunk | while | flops 1617176064 | bytes 12596381 | solution.py:87
  74.8 0.1 dynamic_slice.35
  74.9 0.1 add_select_fusion.3
  75.0 4.7 %select_add_fusion.2 = f32[3072,512]{1,0:T(8,128)} fusion(f32[3072,512]{1,0:T(8,128)} %get-tuple-element.231, s32[512]{0:T(512)S(1)} %get-tuple-element.220, pred[]{:T(512)S(6)} %compare.23, bf16[512]{0:T(512)(128)(2,1)S(1)} %dynamic_slice.35, s32[512]{0:T(512)S(1)} %get-tuple-element.221), kind=kOutput, calls=%fused_computation.3.clone.1 | convolution fusion | flops 1617166336 | bytes 12588033 | tf_op jit(solution)/shard_map/while/body/eval_jaxpr/dot_general | solution.py:83
  79.8 0.1 add_select_fusion.3
  79.9 7.5 %select_add_fusion.2 = f32[3072,512]{1,0:T(8,128)} fusion(f32[3072,512]{1,0:T(8,128)} %get-tuple-element.231, s32[512]{0:T(512)S(1)} %get-tuple-element.220, pred[]{:T(512)S(6)} %compare.23, bf16[512]{0:T(512)(128)(2,1)S(1)} %dynamic_slice.35, s32[512]{0:T(512)S(1)} %get-tuple-element.221), kind=kOutput, calls=%fused_computation.3.clone.1 | convolution fusion | flops 1617166336 | bytes 12588033 | tf_op jit(solution)/shard_map/while/body/eval_jaxpr/dot_general | solution.py:83
  87.4 0.1 add_select_fusion.3
  87.5 7.5 %select_add_fusion.2 = f32[3072,512]{1,0:T(8,128)} fusion(f32[3072,512]{1,0:T(8,128)} %get-tuple-element.231, s32[512]{0:T(512)S(1)} %get-tuple-element.220, pred[]{:T(512)S(6)} %compare.23, bf16[512]{0:T(512)(128)(2,1)S(1)} %dynamic_slice.35, s32[512]{0:T(512)S(1)} %get-tuple-element.221), kind=kOutput, calls=%fused_computation.3.clone.1 | convolution fusion | flops 1617166336 | bytes 12588033 | tf_op jit(solution)/shard_map/while/body/eval_jaxpr/dot_general | solution.py:83
  95.1 0.1 add_select_fusion.3
  95.2 7.5 %select_add_fusion.2 = f32[3072,512]{1,0:T(8,128)} fusion(f32[3072,512]{1,0:T(8,128)} %get-tuple-element.231, s32[512]{0:T(512)S(1)} %get-tuple-element.220, pred[]{:T(512)S(6)} %compare.23, bf16[512]{0:T(512)(128)(2,1)S(1)} %dynamic_slice.35, s32[512]{0:T(512)S(1)} %get-tuple-element.221), kind=kOutput, calls=%fused_computation.3.clone.1 | convolution fusion | flops 1617166336 | bytes 12588033 | tf_op jit(solution)/shard_map/while/body/eval_jaxpr/dot_general | solution.py:83
  102.8 0.1 add_select_fusion.3
  102.9 7.5 %select_add_fusion.2 = f32[3072,512]{1,0:T(8,128)} fusion(f32[3072,512]{1,0:T(8,128)} %get-tuple-element.231, s32[512]{0:T(512)S(1)} %get-tuple-element.220, pred[]{:T(512)S(6)} %compare.23, bf16[512]{0:T(512)(128)(2,1)S(1)} %dynamic_slice.35, s32[512]{0:T(512)S(1)} %get-tuple-element.221), kind=kOutput, calls=%fused_computation.3.clone.1 | convolution fusion | flops 1617166336 | bytes 12588033 | tf_op jit(solution)/shard_map/while/body/eval_jaxpr/dot_general | solution.py:83
  110.5 0.1 add_select_fusion.3
  110.6 7.5 %select_add_fusion.2 = f32[3072,512]{1,0:T(8,128)} fusion(f32[3072,512]{1,0:T(8,128)} %get-tuple-element.231, s32[512]{0:T(512)S(1)} %get-tuple-element.220, pred[]{:T(512)S(6)} %compare.23, bf16[512]{0:T(512)(128)(2,1)S(1)} %dynamic_slice.35, s32[512]{0:T(512)S(1)} %get-tuple-element.221), kind=kOutput, calls=%fused_computation.3.clone.1 | convolution fusion | flops 1617166336 | bytes 12588033 | tf_op jit(solution)/shard_map/while/body/eval_jaxpr/dot_general | solution.py:83
  118.1 0.1 add_select_fusion.3
  118.2 7.5 %select_add_fusion.2 = f32[3072,512]{1,0:T(8,128)} fusion(f32[3072,512]{1,0:T(8,128)} %get-tuple-element.231, s32[512]{0:T(512)S(1)} %get-tuple-element.220, pred[]{:T(512)S(6)} %compare.23, bf16[512]{0:T(512)(128)(2,1)S(1)} %dynamic_slice.35, s32[512]{0:T(512)S(1)} %get-tuple-element.221), kind=kOutput, calls=%fused_computation.3.clone.1 | convolution fusion | flops 1617166336 | bytes 12588033 | tf_op jit(solution)/shard_map/while/body/eval_jaxpr/dot_general | solution.py:83
  125.8 0.1 add_select_fusion.3
  125.9 7.5 %select_add_fusion.2 = f32[3072,512]{1,0:T(8,128)} fusion(f32[3072,512]{1,0:T(8,128)} %get-tuple-element.231, s32[512]{0:T(512)S(1)} %get-tuple-element.220, pred[]{:T(512)S(6)} %compare.23, bf16[512]{0:T(512)(128)(2,1)S(1)} %dynamic_slice.35, s32[512]{0:T(512)S(1)} %get-tuple-element.221), kind=kOutput, calls=%fused_computation.3.clone.1 | convolution fusion | flops 1617166336 | bytes 12588033 | tf_op jit(solution)/shard_map/while/body/eval_jaxpr/dot_general | solution.py:83
  133.4 2.7 %slice.32 = bf16[1024,512]{1,0:T(8,128)(2,1)} slice(f32[3072,512]{1,0:T(8,128)} %get-tuple-element.159), slice={[2048:3072], [0:512]} | slice | bytes 2097152 | tf_op jit(solution)/shard_map/slice | solution.py:113
  136.2 3.9 %all_to_all.40 = f32[2,64,1,512]{3,1,2,0:T(8,128)S(1)} all-to-all(f32[2,64,1,512]{3,1,2,0:T(8,128)S(1)} %pad_maximum_fusion), channel_id=1, replica_groups=mesh['row_0'=4,'row_1'=2,'col_0'=4,'col_1'=4] {'row_1'}, dimensions={0} | all-to-all | bytes 524288 | tf_op jit(solution)/shard_map/all_to_all | solution.py:42
  140.1 5.5 %all-to-all-start.7 = ((bf16[16,64,512]{2,1,0:T(8,128)(2,1)}), bf16[16,64,512]{2,1,0:T(8,128)(2,1)S(1)}, u32[]{:S(2)}, u32[]{:S(2)}) async-start(bf16[16,64,512]{2,1,0:T(8,128)(2,1)} %bitcast.20), calls=%async_computation.7 | async-start | bytes 2097152 | tf_op jit(solution)/shard_map/all_to_all | solution.py:56
  145.6 0.2 copy.22
  145.8 0.2 copy.23
  146.0 0.1 reshape_reshape.12
  146.1 0.2 fusion.18
  146.3 0.2 fusion.17
  146.5 0.7 reduce_sum.18
  147.8 2.7 %slice_multiply_fusion = f32[2048,512]{1,0:T(8,128)S(1)} fusion(f32[3072,512]{1,0:T(8,128)} %get-tuple-element.159, f32[]{:T(128)S(6)} %div.35), kind=kLoop, calls=%fused_computation.20 | loop fusion | flops 1048576 | bytes 8388612 | tf_op jit(solution)/shard_map/mul | solution.py:118
  150.5 0.2 convolution_bitcast_fusion
  150.7 0.1 dynamic_slice.23
  150.8 0.2 fusion.16
  151.0 2.6 %maximum_log_fusion = f32[4,512,512]{2,1,0:T(8,128)} fusion(f32[4,512,512]{2,1,0:T(8,128)S(1)} %bitcast.61, f32[4,512]{1,0:T(4,128)S(1)} %fusion.17, f32[4,512]{1,0:T(4,128)S(1)} %fusion.16), kind=kLoop, calls=%fused_computation.19 | loop fusion | flops 3145728 | bytes 8404992 | tf_op jit(solution)/shard_map/log | solution.py:117
  153.7 10.0 %all-to-all-done.7 = bf16[16,64,512]{2,1,0:T(8,128)(2,1)S(1)} async-done(((bf16[16,64,512]{2,1,0:T(8,128)(2,1)}), bf16[16,64,512]{2,1,0:T(8,128)(2,1)S(1)}, u32[]{:S(2)}, u32[]{:S(2)}) %all-to-all-start.7) | async-done | bytes 1048608 | tf_op jit(solution)/shard_map/all_to_all | solution.py:56
  163.7 0.1 convert_reduce_fusion
  163.9 0.9 fusion.14
  (16 shorter events, 0.6 us)
Async XLA Ops:
  2.0 20.6 %all-to-all-start.5 = ((s32[128,1,1,1]{3,2,1,0:T(1,128)}), s32[128,1,1,1]{3,2,1,0:T(1,128)S(1)}, u32[]{:S(2)}, u32[]{:S(2)}) async-start(s32[128,1,1,1]{3,2,1,0:T(1,128)} %copy.20), calls=%async_computation.5 | async-start | bytes 131072 | tf_op jit(solution)/shard_map/all_to_all | solution.py:33
  23.9 8.5 %all-to-all-start = ((f32[4,1,1,512]{3,2,1,0:T(1,128)}), f32[4,1,1,512]{3,2,1,0:T(1,128)S(1)}, u32[]{:S(2)}, u32[]{:S(2)}) async-start(f32[4,1,1,512]{3,2,1,0:T(1,128)} %stack.12), calls=%async_computation | async-start | bytes 16384 | tf_op jit(solution)/shard_map/all_to_all | solution.py:42
  32.5 14.0 %all-to-all-start.6 = ((bf16[128,1,1,32]{3,2,1,0:T(2,128)(2,1)}), bf16[128,1,1,32]{3,2,1,0:T(2,128)(2,1)S(1)}, u32[]{:S(2)}, u32[]{:S(2)}) async-start(bf16[128,1,1,32]{3,2,1,0:T(2,128)(2,1)} %reshape_transpose_transpose_reshape_reshape_reshape.12), calls=%async_computation.6 | async-start | bytes 131072 | tf_op jit(solution)/shard_map/all_to_all | solution.py:33
  46.5 15.0 %all-to-all-start.4 = ((s32[128,1,1,32]{3,2,1,0:T(1,128)}), s32[128,1,1,32]{3,2,1,0:T(1,128)S(1)}, u32[]{:S(2)}, u32[]{:S(2)}) async-start(s32[128,1,1,32]{3,2,1,0:T(1,128)} %bitcast.2), calls=%async_computation.4 | async-start | bytes 131072 | tf_op jit(solution)/shard_map/all_to_all | solution.py:33
  62.1 8.7 %all-to-all-start.1 = ((f32[4,4,1,512]{3,1,2,0:T(4,128)}), f32[4,4,1,512]{3,1,2,0:T(4,128)S(1)}, u32[]{:S(2)}, u32[]{:S(2)}) async-start(f32[4,4,1,512]{3,1,2,0:T(4,128)} %stack.13), calls=%async_computation.1 | async-start | bytes 65536 | tf_op jit(solution)/shard_map/all_to_all | solution.py:42
  71.4 64.7 %all-to-all-start.2 = ((f32[4,16,1,512]{3,1,2,0:T(8,128)}), f32[4,16,1,512]{3,1,2,0:T(8,128)S(1)}, u32[]{:S(2)}, u32[]{:S(2)}) async-start(f32[4,16,1,512]{3,1,2,0:T(8,128)} %stack.14), calls=%async_computation.2 | async-start | bytes 262144 | tf_op jit(solution)/shard_map/all_to_all | solution.py:42
  140.1 23.6 %all-to-all-start.7 = ((bf16[16,64,512]{2,1,0:T(8,128)(2,1)}), bf16[16,64,512]{2,1,0:T(8,128)(2,1)S(1)}, u32[]{:S(2)}, u32[]{:S(2)}) async-start(bf16[16,64,512]{2,1,0:T(8,128)(2,1)} %bitcast.20), calls=%async_computation.7 | async-start | bytes 2097152 | tf_op jit(solution)/shard_map/all_to_all | solution.py:56
